TPU v7x, 256 devices: a whole 4x4x8 slice. The times are simulated.
256 devices in a mesh: dp: 64 (over x, z, core), mp: 4 (over y).
Axes of the slice: x: 4, y: 4, z: 8, core: 2. Of those that a mesh axis runs over, the one named last changes fastest.
Arguments:
- features: bfloat16 [16384, 512], P('dp'), may hold values from -6 to 6
- adjacency: bfloat16 [4096, 4, 128, 128], P('dp'), may hold values from -0.125 to 0.125
- source_block: int32 [4096, 4], P('dp'), may hold values from 0 to 1
- edge_type: int32 [4096, 4], P('dp'), may hold values from 0 to 19
- target_block: int32 [4096, 4], P('dp'), may hold values from 0 to 1
- live_count: int32 [64, 64], P('dp'), may hold values from 3 to 4, as said below
- relation_weight: bfloat16 [20, 512, 512], P(None, None, 'mp'), may hold values from -0.25 to 0.25
- self_weight: bfloat16 [512, 512], P(None, 'mp'), may hold values from -0.25 to 0.25
- layer_bias: bfloat16 [512], P('mp'), may hold values from -3 to 3
- norm_gain: bfloat16 [512], replicated, may hold values from 0.5 to 1.5
Outputs:
- node_states: bfloat16 [16384, 512], P(('dp', 'mp'))
Inputs may be any that keep to these rules, and one draw needn't show every extreme that they name: `source_block`: row s * 64 + d names a block among sender s's 2 blocks. `target_block`: row d * 64 + s names a block among receiver d's 2 blocks. live_count[d, s] live slots from sender s to receiver d, the first ones; some receiver has all 4 slots live from every sender.
All inputs are finite; a program needn't handle non-finite values.
Results may differ from a plain program's by a relative error of at most 0.007.
Values may be sent and summed in bfloat16 or wider, within the bound.
A program may use at most 128 MiB of HBM per device.

v0:
```python
import jax
import jax.numpy as jnp
from jax import lax
from jax.sharding import PartitionSpec as P

BLK = 128
epsilon = 1e-05


def sent_together(arrays, axis, split_dim, concat_dim, along):
    widths = [a.shape[along] for a in arrays]
    both = jnp.concatenate(arrays, axis=along)
    filled = lax.all_to_all(both, axis, split_axis=split_dim, concat_axis=concat_dim, tiled=True)
    return tuple(jnp.split(filled, [sum(widths[:k]) for k in range(1, len(widths))], axis=along))


def split_up(shard, dim, peers):
    dims = shard.shape
    tiles = shard.reshape(*dims[:dim], peers, dims[dim] // peers, *dims[dim + 1 :])
    return jnp.moveaxis(tiles, dim, 0)


def summed_on_arrival(shard, axis, dim):
    peers = lax.axis_size(axis)
    tiles = lax.all_to_all(split_up(shard, dim, peers), axis, 0, 0, tiled=True)
    return jnp.sum(tiles.astype(jnp.float32), axis=0)


def block_table(features, relation_weight, blocks):
    stacked = features.reshape(blocks, BLK, features.shape[1])
    lookup = jnp.einsum(
        "bid,rdc->bric", stacked, relation_weight, preferred_element_type=jnp.float32
    )
    return lookup.astype(jnp.bfloat16).reshape(
        blocks * relation_weight.shape[0], BLK, relation_weight.shape[2]
    )


def transform_slots(lookup, lookup_rows, adj_tiles):
    chosen = jnp.take(lookup, lookup_rows, axis=0)
    return jnp.einsum("nij,njc->nic", adj_tiles, chosen, preferred_element_type=jnp.float32)


def selector(targets, counts, blocks):
    slot_count = targets.shape[1]
    active = jnp.arange(slot_count, dtype=jnp.int32)[None, :] < counts[:, None]
    matches = targets[:, :, None] == jnp.arange(blocks, dtype=jnp.int32)[None, None, :]
    return jnp.logical_and(matches, active[:, :, None]).astype(jnp.float32)


def per_device(
    features,
    adjacency,
    source_block,
    edge_type,
    target_block,
    live_count,
    relation_weight,
    self_weight,
    layer_bias,
    norm_gain,
):
    peer_count = lax.axis_size("dp")
    slot_count = source_block.shape[1]
    node_rows = features.shape[0]
    blocks = node_rows // BLK
    columns = relation_weight.shape[2]
    lookup = block_table(features, relation_weight, blocks)
    lookup_rows = (source_block * relation_weight.shape[0] + edge_type).reshape(
        peer_count * slot_count
    )
    flat_tiles = adjacency.reshape(peer_count * slot_count, BLK, BLK)
    routed, routed_count = sent_together(
        (target_block, live_count.reshape(peer_count, 1)), "dp", 0, 0, 1
    )
    weights = selector(routed, routed_count[:, 0], blocks)
    receivers = node_rows * lax.axis_size("dp") // node_rows
    message = transform_slots(lookup, lookup_rows, flat_tiles).reshape(
        receivers, slot_count, BLK * columns
    )
    summed = jnp.einsum("rkb,rkx->rbx", weights, message, precision=lax.Precision.HIGHEST)
    aggregate = summed_on_arrival(
        summed.reshape(receivers * blocks * BLK, columns).astype(jnp.bfloat16), "dp", 0
    )
    own_term = jnp.dot(features, self_weight, preferred_element_type=jnp.float32)
    hidden = jax.nn.relu(own_term + aggregate + layer_bias.astype(jnp.float32)).astype(jnp.bfloat16)
    by_rows = lax.all_to_all(hidden, "mp", split_axis=0, concat_axis=1, tiled=True)
    values = by_rows.astype(jnp.float32)
    inverse_rms = lax.rsqrt(jnp.mean(values * values, axis=1, keepdims=True) + epsilon)
    return (values * inverse_rms * norm_gain.astype(jnp.float32)).astype(jnp.bfloat16)


def solution(mesh):
    return jax.shard_map(
        per_device,
        mesh=mesh,
        in_specs=(
            P("dp", None),
            P("dp", None, None, None),
            P("dp", None),
            P("dp", None),
            P("dp", None),
            P("dp", None),
            P(None, None, "mp"),
            P(None, "mp"),
            P("mp"),
            P(),
        ),
        out_specs=P(("dp", "mp"), None),
        check_vma=False,
    )
```

profile of v0, /device:TPU:1, one launch (start us, length us, event | category | flops | bytes accessed | tf_op | source)
XLA Modules:
  0.0 229.2 jit_solution(922433717765947294)
XLA Ops:
  0.0 0.0 copy-start
  0.0 0.9 pad_add_fusion
  0.9 0.7 copy.40
  1.6 13.0 %all-to-all-start = ((s32[64,1,5]{2,1,0:T(1,128)}), s32[64,1,5]{2,1,0:T(1,128)S(1)}, u32[]{:S(2)}, u32[]{:S(2)}) async-start(s32[64,1,5]{2,1,0:T(1,128)} %bitcast.1), calls=%async_computation | async-start | bytes 65536 | tf_op jit(solution)/shard_map/all_to_all | solution.py:13
  14.6 0.7 multiply_add_fusion
  15.3 0.1 copy.41
  15.4 0.1 reshape.102
  15.5 0.1 reshape.99
  15.6 0.0 copy-done
  15.6 2.9 %fusion.8 = bf16[2,20,128,128]{2,3,0,1:T(8,128)(2,1)} fusion(bf16[2,128,512,1]{2,1,0,3:T(8,128)(2,1)} %bitcast.41, bf16[20,512,128]{2,1,0:T(8,128)(2,1)S(1)} %copy-done), kind=kOutput, calls=%fused_computation.10 | convolution fusion | flops 671744000 | bytes 4194304 | tf_op jit(solution)/shard_map/bid,rdc->bric/dot_general | solution.py:31
  18.5 1.8 copy.43
  20.3 8.6 %gather_fusion = bf16[256,128,128]{2,1,0:T(8,128)(2,1)} fusion(bf16[40,128,128]{2,1,0:T(8,128)(2,1)S(1)} %bitcast.39, s32[1024]{0:T(1024)S(1)} %pad_clamp_fusion), kind=kCustom, calls=%fused_computation | custom fusion | bytes 16778240 | tf_op jit(solution)/shard_map/jit(_take)/gather | solution.py:40
  28.9 13.2 %convolution_bitcast_fusion = f32[256,128,128]{1,2,0:T(8,128)} fusion(bf16[256,128,128]{2,1,0:T(8,128)(2,1)} %bitcast.40, bf16[256,128,128]{2,1,0:T(8,128)(2,1)} %gather_fusion, pred[256]{0:T(512)(128)(4,1)S(1)} %compare_and_fusion), kind=kOutput, calls=%fused_computation.2 | convolution fusion | flops 1077936128 | bytes 33554688 | tf_op jit(solution)/shard_map/nij,njc->nic/dot_general | solution.py:41
  42.1 17.5 %copy.46 = f32[256,128,128]{2,1,0:T(8,128)} copy(f32[256,128,128]{1,2,0:T(8,128)} %convolution_bitcast_fusion) | data formatting | bytes 33554432 | tf_op jit(solution)/shard_map/nij,njc->nic/dot_general | solution.py:41
  59.6 20.2 %reshape.104 = f32[64,4,16384]{2,1,0:T(4,128)} reshape(f32[256,128,128]{2,1,0:T(8,128)} %copy.46) | data formatting | bytes 33554432 | tf_op jit(solution)/shard_map/reshape | solution.py:78
  79.8 0.0 all-to-all-done
  79.8 0.2 slice_reduce_fusion
  80.0 0.1 iota_compare_fusion
  80.1 21.4 %convolution_convert_fusion = bf16[64,2,16384]{2,1,0:T(2,128)(2,1)} fusion(f32[64,4,16384]{2,1,0:T(4,128)} %reshape.104, pred[64,4]{1,0:T(8,128)(4,1)S(1)} %iota_compare_fusion, s32[64,4]{1,0:T(8,128)S(1)} %bitcast.43), kind=kOutput, calls=%fused_computation.1 | convolution fusion | flops 102761472 | bytes 20972800 | tf_op jit(solution)/shard_map/rkb,rkx->rbx/dot_general | solution.py:81
  101.5 8.0 %convert_element_type.45 = bf16[64,256,128]{2,1,0:T(8,128)(2,1)} reshape(bf16[64,2,16384]{2,1,0:T(2,128)(2,1)} %convolution_convert_fusion) | data formatting | bytes 8388608 | tf_op jit(solution)/shard_map/convert_element_type | solution.py:83
  109.5 10.7 %all-to-all-start.1 = ((bf16[64,256,128]{2,1,0:T(8,128)(2,1)}), bf16[64,256,128]{2,1,0:T(8,128)(2,1)}, u32[]{:S(2)}, u32[]{:S(2)}) async-start(bf16[64,256,128]{2,1,0:T(8,128)(2,1)} %convert_element_type.45), calls=%async_computation.1 | async-start | bytes 8388608 | tf_op jit(solution)/shard_map/all_to_all | solution.py:25
  120.1 0.0 copy-done.5
  120.2 95.8 %all-to-all-done.1 = bf16[64,256,128]{2,1,0:T(8,128)(2,1)} async-done(((bf16[64,256,128]{2,1,0:T(8,128)(2,1)}), bf16[64,256,128]{2,1,0:T(8,128)(2,1)}, u32[]{:S(2)}, u32[]{:S(2)}) %all-to-all-start.1) | async-done | bytes 4194336 | tf_op jit(solution)/shard_map/all_to_all | solution.py:25
  216.0 2.8 %convert_reduce_fusion = f32[256,128]{1,0:T(8,128)S(1)} fusion(bf16[64,256,128]{2,1,0:T(8,128)(2,1)} %all-to-all-done.1), kind=kLoop, calls=%fused_computation.3 | loop fusion | flops 4161536 | bytes 4325376 | tf_op jit(solution)/shard_map/reduce_sum | solution.py:26
  218.8 0.0 copy-done.2
  218.8 0.0 copy-done.3
  218.8 0.9 fusion.13
  219.7 4.2 %all-to-all-start.2 = ((bf16[4,64,128]{2,1,0:T(8,128)(2,1)}), bf16[4,64,128]{2,1,0:T(8,128)(2,1)S(1)}, u32[]{:S(2)}, u32[]{:S(2)}) async-start(bf16[4,64,128]{2,1,0:T(8,128)(2,1)} %bitcast.11), calls=%async_computation.2 | async-start | bytes 131072 | tf_op jit(solution)/shard_map/all_to_all | solution.py:87
  223.8 0.0 copy-done.4
  223.8 4.5 %all-to-all-done.2 = bf16[4,64,128]{2,1,0:T(8,128)(2,1)S(1)} async-done(((bf16[4,64,128]{2,1,0:T(8,128)(2,1)}), bf16[4,64,128]{2,1,0:T(8,128)(2,1)S(1)}, u32[]{:S(2)}, u32[]{:S(2)}) %all-to-all-start.2) | async-done | bytes 65568 | tf_op jit(solution)/shard_map/all_to_all | solution.py:87
  228.3 0.1 fusion.14
  228.4 0.7 fusion.16
  (12 shorter events, 0.0 us)
Async XLA Ops:
  0.0 15.6 %copy-start = (bf16[20,512,128]{2,1,0:T(8,128)(2,1)S(1)}, bf16[20,512,128]{2,1,0:T(8,128)(2,1)}, u32[]{:S(2)}) copy-start(bf16[20,512,128]{2,1,0:T(8,128)(2,1)} %param.16) | copy-start | bytes 7864324
  1.6 78.2 %all-to-all-start = ((s32[64,1,5]{2,1,0:T(1,128)}), s32[64,1,5]{2,1,0:T(1,128)S(1)}, u32[]{:S(2)}, u32[]{:S(2)}) async-start(s32[64,1,5]{2,1,0:T(1,128)} %bitcast.1), calls=%async_computation | async-start | bytes 65536 | tf_op jit(solution)/shard_map/all_to_all | solution.py:13
  101.5 18.6 %copy-start.5 = (bf16[128]{0:T(256)(128)(2,1)S(1)}, bf16[128]{0:T(256)(128)(2,1)}, u32[]{:S(2)}) copy-start(bf16[128]{0:T(256)(128)(2,1)} %param.18) | copy-start | bytes 772
  101.5 127.7 %copy-start.1 = (bf16[20,512,128]{2,1,0:T(8,128)(2,1)S(1)}, bf16[20,512,128]{2,1,0:T(8,128)(2,1)}, u32[]{:S(2)}) copy-start(bf16[20,512,128]{2,1,0:T(8,128)(2,1)} %param.16) | copy-start | bytes 7864324
  109.5 109.3 %copy-start.2 = (bf16[256,512]{1,0:T(8,128)(2,1)S(1)}, bf16[256,512]{1,0:T(8,128)(2,1)}, u32[]{:S(2)}) copy-start(bf16[256,512]{1,0:T(8,128)(2,1)} %param.10) | copy-start | bytes 786436
  109.5 109.3 %copy-start.3 = (bf16[512,128]{1,0:T(8,128)(2,1)S(1)}, bf16[512,128]{1,0:T(8,128)(2,1)}, u32[]{:S(2)}) copy-start(bf16[512,128]{1,0:T(8,128)(2,1)} %param.17) | copy-start | bytes 393220
  109.5 114.4 %copy-start.4 = (bf16[512]{0:T(512)(128)(2,1)S(1)}, bf16[512]{0:T(512)(128)(2,1)}, u32[]{:S(2)}) copy-start(bf16[512]{0:T(512)(128)(2,1)} %param.19) | copy-start | bytes 3076
  109.5 106.5 %all-to-all-start.1 = ((bf16[64,256,128]{2,1,0:T(8,128)(2,1)}), bf16[64,256,128]{2,1,0:T(8,128)(2,1)}, u32[]{:S(2)}, u32[]{:S(2)}) async-start(bf16[64,256,128]{2,1,0:T(8,128)(2,1)} %convert_element_type.45), calls=%async_computation.1 | async-start | bytes 8388608 | tf_op jit(solution)/shard_map/all_to_all | solution.py:25
  219.7 8.7 %all-to-all-start.2 = ((bf16[4,64,128]{2,1,0:T(8,128)(2,1)}), bf16[4,64,128]{2,1,0:T(8,128)(2,1)S(1)}, u32[]{:S(2)}, u32[]{:S(2)}) async-start(bf16[4,64,128]{2,1,0:T(8,128)(2,1)} %bitcast.11), calls=%async_computation.2 | async-start | bytes 131072 | tf_op jit(solution)/shard_map/all_to_all | solution.py:87
where the time goes:
time: 230 us; the launch traced here: 229 us
  waiting for transfers between devices  100 us (43%)
  local copies, waits for them, and re-layouts  57.3 us (25%)
  matrix products  38.4 us (17%)
  starting transfers between devices  27.8 us (12%)
  other arithmetic  5.3 us (2%)
    all_to_all x1, waiting for transfers between devices, summed_on_arrival(): tiles = lax.all_to_all(split_up(shard, dim, peers), axis, 0, 0, tiled=True)  95.8 us
    dot_general x1, matrix products, per_device(): jnp.einsum('rkb,rkx->rbx', weights, message, precision=lax.Precision.HIGH...  21.4 us
    reshape x1, local copies, waits for them, and re-layouts, per_device(): transform_slots(lookup, lookup_rows, flat_tiles)  20.2 us
    dot_general x1, local copies, waits for them, and re-layouts, transform_slots(): jnp.einsum('nij,njc->nic', adj_tiles, chosen, preferred_element_type=jnp....  17.5 us
    dot_general x1, matrix products, transform_slots(): jnp.einsum('nij,njc->nic', adj_tiles, chosen, preferred_element_type=jnp....  13.2 us
    all_to_all x1, starting transfers between devices, sent_together(): lax.all_to_all(both, axis, split_axis=split_dim, concat_axis=concat_dim,...  13 us
    all_to_all x1, starting transfers between devices, summed_on_arrival(): tiles = lax.all_to_all(split_up(shard, dim, peers), axis, 0, 0, tiled=True)  10.7 us
    gather x1, local copies, waits for them, and re-layouts, transform_slots(): chosen = jnp.take(lookup, lookup_rows, axis=0)  8.61 us
  transfers between devices with their start and end apart: 3, of which 2 were waited for; matrix products, arithmetic and copies ran while one was open for 28% of the time, Pallas kernels for 0%

commit v1 on v0

--- a/solution.py
+++ b/solution.py
@@ -84,7 +84,10 @@
     )
     own_term = jnp.dot(features, self_weight, preferred_element_type=jnp.float32)
     hidden = jax.nn.relu(own_term + aggregate + layer_bias.astype(jnp.float32)).astype(jnp.bfloat16)
-    by_rows = lax.all_to_all(hidden, "mp", split_axis=0, concat_axis=1, tiled=True)
+    by_rows = jnp.concatenate(
+        lax.all_to_all(jnp.stack(jnp.split(hidden, lax.axis_size("mp"), axis=0)), "mp", 0, 0),
+        axis=1,
+    )
     values = by_rows.astype(jnp.float32)
     inverse_rms = lax.rsqrt(jnp.mean(values * values, axis=1, keepdims=True) + epsilon)
     return (values * inverse_rms * norm_gain.astype(jnp.float32)).astype(jnp.bfloat16)

time: 230 us -> 230 us (level)
  no operation moved by 1% of the time
where the time goes in v1:
time: 230 us; the launch traced here: 229 us
  waiting for transfers between devices  100 us (43%)
  local copies, waits for them, and re-layouts  57.3 us (25%)
  matrix products  37.8 us (16%)
  starting transfers between devices  27.8 us (12%)
  other arithmetic  5.94 us (3%)
    all_to_all x1, waiting for transfers between devices, summed_on_arrival(): tiles = lax.all_to_all(split_up(shard, dim, peers), axis, 0, 0, tiled=True)  95.8 us
    dot_general x1, matrix products, per_device(): jnp.einsum('rkb,rkx->rbx', weights, message, precision=lax.Precision.HIGH...  21.4 us
    reshape x1, local copies, waits for them, and re-layouts, per_device(): transform_slots(lookup, lookup_rows, flat_tiles)  20.2 us
    dot_general x1, local copies, waits for them, and re-layouts, transform_slots(): jnp.einsum('nij,njc->nic', adj_tiles, chosen, preferred_element_type=jnp....  17.5 us
    dot_general x1, matrix products, transform_slots(): jnp.einsum('nij,njc->nic', adj_tiles, chosen, preferred_element_type=jnp....  13.2 us
    all_to_all x1, starting transfers between devices, sent_together(): lax.all_to_all(both, axis, split_axis=split_dim, concat_axis=concat_dim,...  13 us
    all_to_all x1, starting transfers between devices, summed_on_arrival(): tiles = lax.all_to_all(split_up(shard, dim, peers), axis, 0, 0, tiled=True)  10.7 us
    gather x1, local copies, waits for them, and re-layouts, transform_slots(): chosen = jnp.take(lookup, lookup_rows, axis=0)  8.6 us
  transfers between devices with their start and end apart: 3, of which 2 were waited for; matrix products, arithmetic and copies ran while one was open for 28% of the time, Pallas kernels for 0%

profile of v1, /device:TPU:1, one launch (start us, length us, event | category | flops | bytes accessed | tf_op | source)
XLA Modules:
  0.0 229.2 jit_solution(13949549175878680359)
XLA Ops:
  0.0 0.0 copy-start
  0.0 0.9 pad_add_fusion
  0.9 0.7 copy.39
  1.6 13.0 %all-to-all-start = ((s32[64,1,5]{2,1,0:T(1,128)}), s32[64,1,5]{2,1,0:T(1,128)S(1)}, u32[]{:S(2)}, u32[]{:S(2)}) async-start(s32[64,1,5]{2,1,0:T(1,128)} %bitcast.1), calls=%async_computation | async-start | bytes 65536 | tf_op jit(solution)/shard_map/all_to_all | solution.py:13
  14.6 0.7 multiply_add_fusion
  15.3 0.1 copy.40
  15.4 0.1 reshape.101
  15.5 0.1 reshape.98
  15.6 2.9 %fusion.8 = bf16[2,20,128,128]{2,3,0,1:T(8,128)(2,1)} fusion(bf16[2,128,512,1]{2,1,0,3:T(8,128)(2,1)} %bitcast.48, bf16[20,512,128]{2,1,0:T(8,128)(2,1)S(1)} %copy-done), kind=kOutput, calls=%fused_computation.10 | convolution fusion | flops 671744000 | bytes 4194304 | tf_op jit(solution)/shard_map/bid,rdc->bric/dot_general | solution.py:31
  18.5 1.8 copy.42
  20.3 8.6 %gather_fusion = bf16[256,128,128]{2,1,0:T(8,128)(2,1)} fusion(bf16[40,128,128]{2,1,0:T(8,128)(2,1)S(1)} %bitcast.46, s32[1024]{0:T(1024)S(1)} %pad_clamp_fusion), kind=kCustom, calls=%fused_computation | custom fusion | bytes 16778240 | tf_op jit(solution)/shard_map/jit(_take)/gather | solution.py:40
  28.9 13.2 %convolution_bitcast_fusion = f32[256,128,128]{1,2,0:T(8,128)} fusion(bf16[256,128,128]{2,1,0:T(8,128)(2,1)} %bitcast.47, bf16[256,128,128]{2,1,0:T(8,128)(2,1)} %gather_fusion, pred[256]{0:T(512)(128)(4,1)S(1)} %compare_and_fusion), kind=kOutput, calls=%fused_computation.2 | convolution fusion | flops 1077936128 | bytes 33554688 | tf_op jit(solution)/shard_map/nij,njc->nic/dot_general | solution.py:41
  42.1 17.5 %copy.45 = f32[256,128,128]{2,1,0:T(8,128)} copy(f32[256,128,128]{1,2,0:T(8,128)} %convolution_bitcast_fusion) | data formatting | bytes 33554432 | tf_op jit(solution)/shard_map/nij,njc->nic/dot_general | solution.py:41
  59.6 20.2 %reshape.103 = f32[64,4,16384]{2,1,0:T(4,128)} reshape(f32[256,128,128]{2,1,0:T(8,128)} %copy.45) | data formatting | bytes 33554432 | tf_op jit(solution)/shard_map/reshape | solution.py:78
  79.8 0.0 all-to-all-done
  79.8 0.2 slice_reduce_fusion
  80.0 0.1 iota_compare_fusion
  80.1 21.4 %convolution_convert_fusion = bf16[64,2,16384]{2,1,0:T(2,128)(2,1)} fusion(f32[64,4,16384]{2,1,0:T(4,128)} %reshape.103, pred[64,4]{1,0:T(8,128)(4,1)S(1)} %iota_compare_fusion, s32[64,4]{1,0:T(8,128)S(1)} %bitcast.50), kind=kOutput, calls=%fused_computation.1 | convolution fusion | flops 102761472 | bytes 20972800 | tf_op jit(solution)/shard_map/rkb,rkx->rbx/dot_general | solution.py:81
  101.5 8.0 %convert_element_type.45 = bf16[64,256,128]{2,1,0:T(8,128)(2,1)} reshape(bf16[64,2,16384]{2,1,0:T(2,128)(2,1)} %convolution_convert_fusion) | data formatting | bytes 8388608 | tf_op jit(solution)/shard_map/convert_element_type | solution.py:83
  109.5 10.7 %all-to-all-start.1 = ((bf16[64,256,128]{2,1,0:T(8,128)(2,1)}), bf16[64,256,128]{2,1,0:T(8,128)(2,1)}, u32[]{:S(2)}, u32[]{:S(2)}) async-start(bf16[64,256,128]{2,1,0:T(8,128)(2,1)} %convert_element_type.45), calls=%async_computation.1 | async-start | bytes 8388608 | tf_op jit(solution)/shard_map/all_to_all | solution.py:25
  120.2 95.8 %all-to-all-done.1 = bf16[64,256,128]{2,1,0:T(8,128)(2,1)} async-done(((bf16[64,256,128]{2,1,0:T(8,128)(2,1)}), bf16[64,256,128]{2,1,0:T(8,128)(2,1)}, u32[]{:S(2)}, u32[]{:S(2)}) %all-to-all-start.1) | async-done | bytes 4194336 | tf_op jit(solution)/shard_map/all_to_all | solution.py:25
  216.0 2.8 %convert_reduce_fusion = f32[256,128]{1,0:T(8,128)S(1)} fusion(bf16[64,256,128]{2,1,0:T(8,128)(2,1)} %all-to-all-done.1), kind=kLoop, calls=%fused_computation.3 | loop fusion | flops 4161536 | bytes 4325376 | tf_op jit(solution)/shard_map/reduce_sum | solution.py:26
  218.8 0.0 copy-done.2
  218.8 0.0 copy-done.3
  218.8 0.2 fusion.13
  219.1 0.6 pad_maximum_fusion
  219.7 4.2 %all-to-all-start.2 = ((bf16[4,64,128]{2,1,0:T(8,128)(2,1)}), bf16[4,64,128]{2,1,0:T(8,128)(2,1)S(1)}, u32[]{:S(2)}, u32[]{:S(2)}) async-start(bf16[4,64,128]{2,1,0:T(8,128)(2,1)} %pad_maximum_fusion), calls=%async_computation.2 | async-start | bytes 131072 | tf_op jit(solution)/shard_map/all_to_all | solution.py:88
  223.9 0.0 copy-done.4
  223.9 4.5 %all-to-all-done.2 = bf16[4,64,128]{2,1,0:T(8,128)(2,1)S(1)} async-done(((bf16[4,64,128]{2,1,0:T(8,128)(2,1)}), bf16[4,64,128]{2,1,0:T(8,128)(2,1)S(1)}, u32[]{:S(2)}, u32[]{:S(2)}) %all-to-all-start.2) | async-done | bytes 65568 | tf_op jit(solution)/shard_map/all_to_all | solution.py:88
  228.4 0.1 fusion.14
  228.5 0.7 fusion.16
  229.2 0.0 copy-done.1
  (14 shorter events, 0.1 us)
Async XLA Ops:
  0.0 15.6 %copy-start = (bf16[20,512,128]{2,1,0:T(8,128)(2,1)S(1)}, bf16[20,512,128]{2,1,0:T(8,128)(2,1)}, u32[]{:S(2)}) copy-start(bf16[20,512,128]{2,1,0:T(8,128)(2,1)} %param.16) | copy-start | bytes 7864324
  1.6 78.2 %all-to-all-start = ((s32[64,1,5]{2,1,0:T(1,128)}), s32[64,1,5]{2,1,0:T(1,128)S(1)}, u32[]{:S(2)}, u32[]{:S(2)}) async-start(s32[64,1,5]{2,1,0:T(1,128)} %bitcast.1), calls=%async_computation | async-start | bytes 65536 | tf_op jit(solution)/shard_map/all_to_all | solution.py:13
  101.5 18.6 %copy-start.5 = (bf16[128]{0:T(256)(128)(2,1)S(1)}, bf16[128]{0:T(256)(128)(2,1)}, u32[]{:S(2)}) copy-start(bf16[128]{0:T(256)(128)(2,1)} %param.18) | copy-start | bytes 772
  101.5 127.7 %copy-start.1 = (bf16[20,512,128]{2,1,0:T(8,128)(2,1)S(1)}, bf16[20,512,128]{2,1,0:T(8,128)(2,1)}, u32[]{:S(2)}) copy-start(bf16[20,512,128]{2,1,0:T(8,128)(2,1)} %param.16) | copy-start | bytes 7864324
  109.5 109.3 %copy-start.2 = (bf16[256,512]{1,0:T(8,128)(2,1)S(1)}, bf16[256,512]{1,0:T(8,128)(2,1)}, u32[]{:S(2)}) copy-start(bf16[256,512]{1,0:T(8,128)(2,1)} %param.10) | copy-start | bytes 786436
  109.5 109.3 %copy-start.3 = (bf16[512,128]{1,0:T(8,128)(2,1)S(1)}, bf16[512,128]{1,0:T(8,128)(2,1)}, u32[]{:S(2)}) copy-start(bf16[512,128]{1,0:T(8,128)(2,1)} %param.17) | copy-start | bytes 393220
  109.5 114.4 %copy-start.4 = (bf16[512]{0:T(512)(128)(2,1)S(1)}, bf16[512]{0:T(512)(128)(2,1)}, u32[]{:S(2)}) copy-start(bf16[512]{0:T(512)(128)(2,1)} %param.19) | copy-start | bytes 3076
  109.5 106.5 %all-to-all-start.1 = ((bf16[64,256,128]{2,1,0:T(8,128)(2,1)}), bf16[64,256,128]{2,1,0:T(8,128)(2,1)}, u32[]{:S(2)}, u32[]{:S(2)}) async-start(bf16[64,256,128]{2,1,0:T(8,128)(2,1)} %convert_element_type.45), calls=%async_computation.1 | async-start | bytes 8388608 | tf_op jit(solution)/shard_map/all_to_all | solution.py:25
  219.7 8.7 %all-to-all-start.2 = ((bf16[4,64,128]{2,1,0:T(8,128)(2,1)}), bf16[4,64,128]{2,1,0:T(8,128)(2,1)S(1)}, u32[]{:S(2)}, u32[]{:S(2)}) async-start(bf16[4,64,128]{2,1,0:T(8,128)(2,1)} %pad_maximum_fusion), calls=%async_computation.2 | async-start | bytes 131072 | tf_op jit(solution)/shard_map/all_to_all | solution.py:88
